TPU v7x, 32 devices: a whole 2x2x4 slice. The times are simulated.
32 devices in a mesh: prow: 8 (over y, x, core), pcol: 4 (over z).
Axes of the slice: x: 2, y: 2, z: 4, core: 2. Of those that a mesh axis runs over, the one named last changes fastest.
Arguments:
- ancestor_inverse: float32 [8, 8, 512, 512], P('prow', 'pcol'), may hold values from -0.09375 to 0.09375
- factor_panel: float32 [512, 8, 3, 512], P('pcol', 'prow'), may hold values from -0.75 to 0.75
- pivot_inverse: float32 [3, 512, 512], P(None, 'prow', 'pcol'), may hold values from -6 to 6
- structure: int32 [8, 3], replicated, may hold values from 0 to 1, as said below
Outputs:
- inverse_panel: float32 [512, 8, 3, 512], P('pcol', 'prow')
- diagonal_block: float32 [3, 512, 512], P(None, 'prow', 'pcol')
Inputs may be any that keep to these rules, and one draw needn't show every extreme that they name: structure[J, K] is 1 where ancestor J lies in supernode K's structure and 0 elsewhere; the last ancestor, 7, lies in every supernode's structure.
All inputs are finite; a program needn't handle non-finite values.
Results may differ from a plain program's by a relative error of at most 0.00007.
Values sent between devices are 32-bit elements; how exact they have to be, the bound alone decides.
A program may use at most 64 MiB of HBM per device.

v0:
```python
import jax
import jax.numpy as jnp
from jax import lax
from jax.sharding import PartitionSpec as P


def spread(value, axis, source):
    kept = jnp.where(lax.axis_index(axis) == source, value, 0).astype(value.dtype)
    return lax.psum(kept, axis)


def keep_same(running):
    return running


def body(ancestor_inverse, factor_panel, pivot_inverse, structure):
    row_count = ancestor_inverse.shape[0]
    col_count = ancestor_inverse.shape[1]
    width = ancestor_inverse.shape[3]
    ratio = lax.axis_size("prow") // lax.axis_size("pcol")
    grid_row = lax.axis_index("prow")
    grid_col = lax.axis_index("pcol")
    struct_float = structure.astype(jnp.float32)
    own_mask = lax.dynamic_slice_in_dim(struct_float, grid_row * row_count, row_count, 0)
    col_mask = lax.dynamic_slice_in_dim(structure, grid_col * col_count, col_count, 0)
    row_panel = lax.all_gather(factor_panel, "pcol", axis=0, tiled=True)
    pieces = []
    for member in range(ratio):
        pieces.append(spread(row_panel, "prow", grid_col * ratio + member))
    columns = jnp.concatenate(pieces, axis=1)
    count_here = columns.shape[2]
    running = jnp.zeros(
        (lax.axis_size("pcol") * (width // lax.axis_size("pcol")), row_count, count_here, width),
        jnp.float32,
    )
    for member in range(col_count):
        for super_index in range(count_here):

            def add_block(
                total,
                inverse_block=ancestor_inverse[0, member],
                factor_block=columns[:, member, super_index, :],
                position=super_index,
                row_at=0,
            ):
                update = jnp.dot(
                    inverse_block,
                    factor_block,
                    precision=lax.Precision.HIGHEST,
                    preferred_element_type=jnp.float32,
                )
                return total.at[:, row_at, position, :].add(update)

            needed = jnp.logical_and(
                col_mask[member, super_index] > 0, own_mask[0, super_index] > 0
            )
            running = lax.cond(needed, add_block, keep_same, running)
    share = lax.psum_scatter(running, "pcol", scatter_dimension=0, tiled=True)
    diagonal_term = None
    share, diagonal_term = (share, diagonal_term)
    inverse_panel = -own_mask[None, :, :, None] * share
    local_rows = factor_panel * own_mask[None, :, :, None]
    diagonal_term = jnp.einsum(
        "riKa,riKb->Kab",
        local_rows,
        inverse_panel,
        precision=lax.Precision.HIGHEST,
        preferred_element_type=jnp.float32,
    )
    by_rows = lax.psum_scatter(diagonal_term, "prow", scatter_dimension=1, tiled=True)
    by_both = lax.psum_scatter(by_rows, "pcol", scatter_dimension=2, tiled=True)
    return (inverse_panel, pivot_inverse - by_both)


def solution(mesh):
    placed = (
        P("prow", "pcol", None, None),
        P("pcol", "prow", None, None),
        P(None, "prow", "pcol"),
        P(),
    )
    return jax.shard_map(
        body,
        mesh=mesh,
        in_specs=placed,
        out_specs=(P("pcol", "prow", None, None), P(None, "prow", "pcol")),
        check_vma=False,
    )
```

profile of v0, /device:TPU:0, one launch (start us, length us, event | category | flops | bytes accessed | tf_op | source)
XLA Modules:
  0.0 372.1 jit_solution(6345583255996827414)
XLA Ops:
  7.2 0.0 all-gather.2.cloned.1.call-start
  7.2 0.7 all-gather.2.cloned.1.call-update
  7.9 0.0 all-reduce.4.cloned.1.call-start
  8.0 67.8 %all-gather.2.cloned.1.call-done = f32[512,1,3,512]{3,1,2,0:T(1,128)} async-done(((f32[128,1,3,512]{3,1,2,0:T(1,128)}), f32[512,1,3,512]{3,1,2,0:T(1,128)}) %all-gather.2.cloned.1.call-update) | async-done | bytes 3145744 | tf_op jit(solution)/shard_map/all_gather | solution.py:26
  75.7 8.9 %broadcast_select_fusion = (f32[512,1,3,512]{3,1,2,0:T(1,128)}, f32[512,1,3,512]{3,1,2,0:T(1,128)}) fusion(f32[512,1,3,512]{3,1,2,0:T(1,128)} %all-gather.2.cloned.1.call-done, pred[]{:T(512)S(6)} %eq.7, pred[]{:T(512)S(6)} %eq.6), kind=kLoop, calls=%fused_computation.32 | loop fusion | flops 1572864 | bytes 9437186 | tf_op jit(solution)/shard_map/jit(_where)/select_n | solution.py:8
  84.6 0.0 copy-start.9
  84.6 0.0 copy-start.7
  84.6 0.0 all-reduce.4.cloned.1.call-update
  84.7 0.0 reduce-scatter.4.cloned.1.call-start
  84.7 0.6 copy-done.9
  85.3 0.1 constant_dynamic-slice_fusion
  85.4 0.7 fusion.25
  86.7 0.2 fusion.24
  86.9 0.6 fusion.26
  92.5 0.0 copy-done.7
  92.5 1.5 slice_bitcast_fusion
  94.0 93.5 %all-reduce.4.cloned.1.call-done = (f32[512,1,3,512]{3,1,2,0:T(1,128)}, f32[512,1,3,512]{3,1,2,0:T(1,128)}) async-done(((f32[512,1,3,512]{3,1,2,0:T(1,128)}, f32[512,1,3,512]{3,1,2,0:T(1,128)}), (f32[512,1,3,512]{3,1,2,0:T(1,128)}, f32[512,1,3,512]{3,1,2,0:T(1,128)})) %all-reduce.4.cloned.1.call-update) | async-done | bytes 6291472 | tf_op jit(solution)/shard_map/psum | solution.py:9
  187.4 0.4 conditional.6
  187.4 0.4 broadcast_in_dim.10
  187.8 0.2 conditional.7
  188.0 0.2 conditional.9
  188.3 0.3 conditional.11
  188.6 0.0 copy-start
  188.6 1.6 copy-done
  190.2 0.0 reduce-scatter.4.cloned.1.call-update
  190.2 0.0 reduce-scatter.6.cloned.1.call-start
  190.3 97.8 %reduce-scatter.4.cloned.1.call-done = f32[128,1,3,512]{3,0,2,1:T(8,128)} async-done(((f32[512,1,3,512]{3,0,2,1:T(8,128)}), f32[128,1,3,512]{3,0,2,1:T(8,128)}) %reduce-scatter.4.cloned.1.call-update) | async-done | bytes 786448 | tf_op jit(solution)/shard_map/reduce_scatter | solution.py:58
  288.0 1.3 broadcast_multiply_fusion
  289.3 5.5 %fusion.20 = f32[3,512,512]{2,1,0:T(8,128)} fusion(f32[128,1,3,512]{3,0,2,1:T(8,128)S(1)} %broadcast_multiply_fusion, f32[128,1,3,512]{3,1,2,0:T(1,128)} %param.29, f32[3]{0:T(128)S(1)} %get-tuple-element.183), kind=kOutput, calls=%fused_computation.36 | convolution fusion | flops 1208156160 | bytes 4718604 | tf_op jit(solution)/shard_map/riKa,riKb->Kab/dot_general | solution.py:63
  294.8 0.0 copy-start.8
  294.8 0.0 reduce-scatter.6.cloned.1.call-update
  294.8 0.0 reduce-scatter.8.cloned.1.call-start
  294.9 46.0 %reduce-scatter.6.cloned.1.call-done = f32[3,64,512]{2,1,0:T(8,128)} async-done(((f32[3,512,512]{2,1,0:T(8,128)}), f32[3,64,512]{2,1,0:T(8,128)}) %reduce-scatter.6.cloned.1.call-update) | async-done | bytes 393232 | tf_op jit(solution)/shard_map/reduce_scatter | solution.py:70
  340.9 0.0 reduce-scatter.8.cloned.1.call-update
  341.0 1.7 copy.22
  342.7 21.4 %reduce-scatter.8.cloned.1.call-done = f32[3,64,128]{2,1,0:T(8,128)} async-done(((f32[3,64,512]{2,1,0:T(8,128)}), f32[3,64,128]{2,1,0:T(8,128)}) %reduce-scatter.8.cloned.1.call-update) | async-done | bytes 98320 | tf_op jit(solution)/shard_map/reduce_scatter | solution.py:71
  364.0 0.0 copy-done.8
  364.0 1.5 sub.3
  (4 shorter events, 0.0 us)
Async XLA Ops:
  7.2 68.6 %all-gather.2.cloned.1.call-start = ((), (), s32[]{:S(2)}) async-start(), calls=%async_computation.3 | async-start | bytes 3932160 | tf_op jit(solution)/shard_map/all_gather | solution.py:26
  7.9 179.5 %all-reduce.4.cloned.1.call-start = ((), (), s32[]{:S(2)}) async-start(), calls=%async_computation.7 | async-start | bytes 12582912 | tf_op jit(solution)/shard_map/psum | solution.py:9
  84.6 0.7 copy-start.9
  84.6 7.8 %copy-start.7 = (f32[1,2,512,512]{3,2,1,0:T(8,128)S(1)}, f32[1,2,512,512]{3,2,1,0:T(8,128)}, u32[]{:S(2)}) copy-start(f32[1,2,512,512]{3,2,1,0:T(8,128)} %param.28) | copy-start | bytes 6291460
  84.7 203.4 %reduce-scatter.4.cloned.1.call-start = ((), (), s32[]{:S(2)}) async-start(), calls=%async_computation.4 | async-start | bytes 3932160 | tf_op jit(solution)/shard_map/reduce_scatter | solution.py:58
  188.6 1.6 copy-start
  190.2 150.7 %reduce-scatter.6.cloned.1.call-start = ((), (), s32[]{:S(2)}) async-start(), calls=%async_computation.5 | async-start | bytes 3538944 | tf_op jit(solution)/shard_map/reduce_scatter | solution.py:70
  294.8 69.2 %copy-start.8 = (f32[3,64,128]{2,1,0:T(8,128)S(1)}, f32[3,64,128]{2,1,0:T(8,128)}, u32[]{:S(2)}) copy-start(f32[3,64,128]{2,1,0:T(8,128)} %param.30) | copy-start | bytes 294916
  294.8 69.2 %reduce-scatter.8.cloned.1.call-start = ((), (), s32[]{:S(2)}) async-start(), calls=%async_computation.6 | async-start | bytes 491520 | tf_op jit(solution)/shard_map/reduce_scatter | solution.py:71
Sparse Core Ops, SparseCore 0:
  9.5 66.1 all-gather.1
  84.8 102.5 all-reduce.3
  190.3 97.6 reduce-scatter.3
  295.0 45.9 reduce-scatter.5
  343.1 20.9 reduce-scatter.7
where the time goes:
time: 379 us; the launch traced here: 372 us
  waiting for transfers between devices  327 us (86%)
  between operations  19.5 us (5%)
  other arithmetic  11.7 us (3%)
  local copies, waits for them, and re-layouts  7.3 us (2%)
  matrix products  5.49 us (1%)
    reduce_scatter x1, waiting for transfers between devices, body(): share = lax.psum_scatter(running, 'pcol', scatter_dimension=0, tiled=True)  97.8 us
    psum x1, waiting for transfers between devices, spread(): return lax.psum(kept, axis)  93.5 us
    all_gather x1, waiting for transfers between devices, body(): row_panel = lax.all_gather(factor_panel, 'pcol', axis=0, tiled=True)  67.8 us
    reduce_scatter x1, waiting for transfers between devices, body(): lax.psum_scatter(diagonal_term, 'prow', scatter_dimension=1, tiled=True)  46 us
    reduce_scatter x1, waiting for transfers between devices, body(): by_both = lax.psum_scatter(by_rows, 'pcol', scatter_dimension=2, tiled=True)  21.4 us
    select_n x1, other arithmetic, spread(): jnp.where(lax.axis_index(axis) == source, value, 0).astype(value.dtype)  8.9 us
  transfers between devices with their start and end apart: 5, of which 5 were waited for; matrix products, arithmetic and copies ran while one was open for 1% of the time, Pallas kernels for 0%

commit v1 on v0

v1 whole, which is shorter than its diff:
```python
import functools

import jax
import jax.numpy as jnp
from jax import lax
from jax.experimental import pallas as pl
from jax.experimental.pallas import tpu as pltpu
from jax.sharding import PartitionSpec as P

MESH = pl.DeviceIdType.MESH
PAIR = 2


def split(value):
    high = value.astype(jnp.bfloat16)
    low = (value - high.astype(jnp.float32)).astype(jnp.bfloat16)
    return high, low


def dot3(a_high, a_low, b_high, b_low, dims):
    def one(a, b):
        return lax.dot_general(a, b, (dims, ((), ())), preferred_element_type=jnp.float32)

    return one(a_high, b_high) + (one(a_high, b_low) + one(a_low, b_high))


def kernel(
    rows_n,
    cols_n,
    struct_ref,
    factor_ref,
    inverse_ref,
    pivot_ref,
    panel_ref,
    diag_ref,
    a_full,
    a_high,
    a_low,
    staged,
    columns,
    l_high,
    l_low,
    partial,
    ring_in,
    terms,
    pair_in,
    pair_sum,
    chip_in,
    cut,
    cut_in,
    a_sem,
    hop_send,
    hop_recv,
    all_send,
    all_recv,
    ring_send,
    ring_recv,
    pair_send,
    pair_recv,
    chip_send,
    chip_recv,
    cut_send,
    cut_recv,
):
    row = lax.axis_index("prow")
    col = lax.axis_index("pcol")
    supers = factor_ref.shape[0]
    members, width = a_full.shape[0], a_full.shape[1]
    rows = factor_ref.shape[1]
    chips = rows_n // PAIR
    part = width // rows_n
    lanes = width // cols_n
    core = lax.rem(row, PAIR)
    chip = row // PAIR
    mate = chip * PAIR + (1 - core)
    group = row // members
    member = lax.rem(row, members)

    def wrap(value, size):
        return lax.rem(value + 4 * size, size)

    barrier = pltpu.get_barrier_semaphore()
    for step in range(1, rows_n):
        pl.semaphore_signal(
            barrier, inc=1, device_id={"prow": lax.rem(row + step, rows_n)}, device_id_type=MESH
        )
    for step in range(1, cols_n):
        pl.semaphore_signal(
            barrier, inc=1, device_id={"pcol": lax.rem(col + step, cols_n)}, device_id_type=MESH
        )
    pl.semaphore_wait(barrier, rows_n + cols_n - 2)

    def remote(src, dst, send, recv, where):
        return pltpu.make_async_remote_copy(
            src_ref=src, dst_ref=dst, send_sem=send, recv_sem=recv, device_id=where, device_id_type=MESH
        )

    class Hop:
        def __init__(self, src, dst, send, recv, where, stays):
            self.far = remote(src, dst, send, recv, where)
            self.near = pltpu.make_async_copy(src, dst, recv)
            self.stays = stays

        def start(self):
            pl.when(self.stays)(self.near.start)
            pl.when(jnp.logical_not(self.stays))(self.far.start)

        def wait_recv(self):
            pl.when(self.stays)(self.near.wait)
            pl.when(jnp.logical_not(self.stays))(self.far.wait_recv)

        def wait_send(self):
            pl.when(jnp.logical_not(self.stays))(self.far.wait_send)

    sent = []

    def across(k):
        to_group = lax.rem(group + col + k, cols_n)
        return Hop(
            factor_ref.at[k],
            staged.at[k],
            hop_send.at[0, k],
            hop_recv.at[0, k],
            {"prow": to_group * members + member},
            lax.rem(col + k, cols_n) == 0,
        )

    def along(k):
        to_col = wrap(group - col - k, cols_n)
        return Hop(
            staged.at[k],
            columns.at[k, member * cols_n + col],
            hop_send.at[1, k],
            hop_recv.at[1, k],
            {"pcol": to_col},
            to_col == col,
        )

    def arrived(k):
        to_col = wrap(group - col - k, cols_n)
        here = columns.at[k, slot_of(row, k)]
        return Hop(staged.at[k], here, hop_send.at[1, k], hop_recv.at[1, k], {"pcol": to_col}, to_col == col)

    def slot_of(source, k):
        return lax.rem(source, members) * cols_n + wrap(source // members - col - k, cols_n)

    def spread(k, index, source, target):
        here = columns.at[k, slot_of(source, k)]
        return remote(here, here, all_send.at[k, index], all_recv.at[k, index], {"prow": target})

    def back(source, step):
        return lax.rem(source - PAIR * step + rows_n, rows_n)

    def start_spread(k):
        arrived(k).wait_recv()
        for step in range(chips - 1, 0, -1):
            copy = spread(k, step, row, lax.rem(row + PAIR * step, rows_n))
            copy.start()
            sent.append(copy)
        copy = spread(k, 0, row, mate)
        copy.start()
        sent.append(copy)

    def forward(k):
        for step in range(1, chips):
            spread(k, step, back(row, step), mate).wait_recv()
            copy = spread(k, chips - 1 + step, back(row, step), mate)
            copy.start()
            sent.append(copy)

    def collect(k):
        spread(k, 0, mate, mate).wait_recv()
        for step in range(1, chips):
            spread(k, chips - 1 + step, back(mate, step), mate).wait_recv()

    def ring_block(step):
        return wrap(col - 1 - step, cols_n)

    def ring_copy(k, step):
        block = pl.ds(pl.multiple_of(ring_block(step) * rows, rows), rows)
        return remote(
            partial.at[k, block],
            ring_in.at[k, step],
            ring_send.at[k, step],
            ring_recv.at[k, step],
            {"pcol": lax.rem(col + 1, cols_n)},
        )

    def multiply(k, step):
        block = pl.ds(pl.multiple_of(ring_block(step) * rows, rows), rows)
        partial[k, block, :] = dot3(
            a_high[block, :], a_low[block, :], l_high[...], l_low[...], ((1,), (0,))
        )

    def start_ring(k):
        collect(k)

        def convert(index, carry):
            mask = struct_ref[col * members + index // cols_n, k].astype(jnp.float32)
            high, low = split(columns[k, index] * mask)
            at = pl.ds(pl.multiple_of(index * rows, rows), rows)
            l_high[at, :] = high
            l_low[at, :] = low
            return carry

        lax.fori_loop(0, members * cols_n, convert, 0)
        multiply(k, 0)
        copy = ring_copy(k, 0)
        copy.start()
        sent.append(copy)

        def others(step, carry):
            multiply(k, step)
            return carry

        lax.fori_loop(1, cols_n, others, 0)

    def ring_step(k, step):
        ring_copy(k, step - 1).wait_recv()
        block = pl.ds(pl.multiple_of(ring_block(step) * rows, rows), rows)
        partial[k, block, :] = partial[k, block, :] + ring_in[k, step - 1]
        copy = ring_copy(k, step)
        copy.start()
        sent.append(copy)

    def pair_copy(k):
        return remote(terms.at[k, 1 - core], pair_in.at[k], pair_send.at[k], pair_recv.at[k], {"prow": mate})

    def chip_copy(k, step):
        to_chip = lax.rem(chip + step, chips)
        return remote(
            pair_sum.at[k, to_chip],
            chip_in.at[k, step - 1],
            chip_send.at[k, step - 1],
            chip_recv.at[k, step - 1],
            {"prow": to_chip * PAIR + core},
        )

    def cut_copy(k, step):
        to_col = lax.rem(col + step, cols_n)
        return remote(
            cut.at[k, to_col],
            cut_in.at[k, step - 1],
            cut_send.at[k, step - 1],
            cut_recv.at[k, step - 1],
            {"pcol": to_col},
        )

    def finish_panel(k):
        ring_copy(k, cols_n - 2).wait_recv()
        block = pl.ds(pl.multiple_of(col * rows, rows), rows)
        mask = struct_ref[row, k].astype(jnp.float32)
        result = -mask * (partial[k, block, :] + ring_in[k, cols_n - 2])
        panel_ref[k] = result
        f_high, f_low = split(factor_ref[k] * mask)
        r_high, r_low = split(result)
        for at in range(rows_n):
            these = slice(at * part, (at + 1) * part)
            terms[k, at % PAIR, at // PAIR] = dot3(
                f_high[:, these], f_low[:, these], r_high, r_low, ((0,), (0,))
            )
        copy = pair_copy(k)
        copy.start()
        sent.append(copy)

    def add_pair(k):
        pair_copy(k).wait_recv()
        pair_sum[k] = terms[k, core] + pair_in[k]
        for step in range(chips - 1, 0, -1):
            copy = chip_copy(k, step)
            copy.start()
            sent.append(copy)

    def add_chips(k):
        total = pair_sum[k, chip]
        for step in range(1, chips):
            chip_copy(k, step).wait_recv()
            total = total + chip_in[k, step - 1]
        for at in range(cols_n):
            cut[k, at] = total[:, at * lanes : (at + 1) * lanes]
        for step in range(cols_n - 1, 0, -1):
            copy = cut_copy(k, step)
            copy.start()
            sent.append(copy)

    def add_cuts(k):
        total = cut[k, col]
        for step in range(1, cols_n):
            cut_copy(k, step).wait_recv()
            total = total + cut_in[k, step - 1]
        diag_ref[k] = pivot_ref[k] - total

    load = pltpu.make_async_copy(inverse_ref.at[0], a_full, a_sem)
    load.start()
    for k in range(supers):
        across(k).start()
        sent.append(across(k))
    for k in range(supers):
        across(k).wait_recv()
        along(k).start()
        sent.append(along(k))
    load.wait()
    for index in range(members):
        high, low = split(a_full[index])
        a_high[:, index * width : (index + 1) * width] = high
        a_low[:, index * width : (index + 1) * width] = low

    start_spread(0)
    stages = [start_ring]
    for step in range(1, cols_n - 1):
        stages.append(functools.partial(lambda at, k: ring_step(k, at), step))
    stages += [finish_panel, add_pair, add_chips, add_cuts]
    for wave in range(supers + len(stages) - 1):
        if wave < supers:
            if wave + 1 < supers:
                start_spread(wave + 1)
            forward(wave)
        for k in range(supers):
            if 0 <= wave - k < len(stages):
                stages[wave - k](k)

    for copy in sent:
        copy.wait_send()


def body(ancestor_inverse, factor_panel, pivot_inverse, structure):
    rows_n, cols_n = lax.axis_size("prow"), lax.axis_size("pcol")
    members, width = ancestor_inverse.shape[1], ancestor_inverse.shape[3]
    rows, _, supers, _ = factor_panel.shape
    chips, part, lanes = rows_n // PAIR, width // rows_n, width // cols_n
    factor = jnp.transpose(factor_panel[:, 0], (1, 0, 2))
    f32, b16, dma = jnp.float32, jnp.bfloat16, pltpu.SemaphoreType.DMA
    vmem = pl.BlockSpec(memory_space=pltpu.VMEM)
    panel, diagonal = pl.pallas_call(
        functools.partial(kernel, rows_n, cols_n),
        out_shape=(
            jax.ShapeDtypeStruct((supers, rows, width), f32),
            jax.ShapeDtypeStruct(pivot_inverse.shape, f32),
        ),
        in_specs=[
            pl.BlockSpec(memory_space=pltpu.SMEM),
            vmem,
            pl.BlockSpec(memory_space=pl.ANY),
            vmem,
        ],
        out_specs=(vmem, vmem),
        scratch_shapes=[
            pltpu.VMEM((members, width, width), f32),
            pltpu.VMEM((width, members * width), b16),
            pltpu.VMEM((width, members * width), b16),
            pltpu.VMEM((supers, rows, width), f32),
            pltpu.VMEM((supers, members * cols_n, rows, width), f32),
            pltpu.VMEM((members * width, width), b16),
            pltpu.VMEM((members * width, width), b16),
            pltpu.VMEM((supers, width, width), f32),
            pltpu.VMEM((supers, cols_n - 1, rows, width), f32),
            pltpu.VMEM((supers, PAIR, chips, part, width), f32),
            pltpu.VMEM((supers, chips, part, width), f32),
            pltpu.VMEM((supers, chips, part, width), f32),
            pltpu.VMEM((supers, chips - 1, part, width), f32),
            pltpu.VMEM((supers, cols_n, part, lanes), f32),
            pltpu.VMEM((supers, cols_n - 1, part, lanes), f32),
            dma,
            dma((2, supers)),
            dma((2, supers)),
            dma((supers, 2 * chips)),
            dma((supers, 2 * chips)),
            dma((supers, cols_n - 1)),
            dma((supers, cols_n - 1)),
            dma((supers,)),
            dma((supers,)),
            dma((supers, chips - 1)),
            dma((supers, chips - 1)),
            dma((supers, cols_n - 1)),
            dma((supers, cols_n - 1)),
        ],
        compiler_params=pltpu.CompilerParams(
            collective_id=0, has_side_effects=True, vmem_limit_bytes=56 * 1024 * 1024
        ),
    )(structure, factor, ancestor_inverse, pivot_inverse)
    return jnp.transpose(panel, (1, 0, 2))[:, None], diagonal


def solution(mesh):
    placed = (
        P("prow", "pcol", None, None),
        P("pcol", "prow", None, None),
        P(None, "prow", "pcol"),
        P(),
    )
    return jax.shard_map(
        body,
        mesh=mesh,
        in_specs=placed,
        out_specs=(P("pcol", "prow", None, None), P(None, "prow", "pcol")),
        check_vma=False,
    )
```

time: 379 us -> 133 us (0.35); the launches traced: 372 us -> 133 us
  waiting for transfers between devices: 327 us -> 0 us
  Pallas kernels: 0 us -> 125 us
  between operations: 19.5 us -> 0.64 us
  other arithmetic: 11.7 us -> 0 us
  matrix products: 5.49 us -> 0 us
    reduce_scatter x3 -> x0, waiting for transfers between devices: 165 us -> none  [the longest x1 97.8 us: body(): share = lax.psum_scatter(running, 'pcol', scatter_dimension=0, tiled=True)]
    pallas_call x0 -> x1, Pallas kernels: none -> 125 us  [body(): pl.pallas_call(functools.partial(kernel, rows_n, cols_n), out_shape=(jax....]
    psum x1 -> x0, waiting for transfers between devices: 93.5 us -> none  [spread(): return lax.psum(kept, axis)]
    all_gather x1 -> x0, waiting for transfers between devices: 67.8 us -> none  [body(): row_panel = lax.all_gather(factor_panel, 'pcol', axis=0, tiled=True)]
    select_n x1 -> x0, other arithmetic: 8.9 us -> none  [spread(): jnp.where(lax.axis_index(axis) == source, value, 0).astype(value.dtype)]
    dot_general x1 -> x0, matrix products: 5.49 us -> none  [body(): jnp.einsum('riKa,riKb->Kab', local_rows, inverse_panel, precision=lax.Pre...]
    unnamed x9 -> x4, local copies, waits for them, and re-layouts: 3.92 us -> 7.79 us
  transfers between devices with their start and end apart: 5 -> 0, of which waited for: 5 -> 0; matrix products, arithmetic and copies ran while one was open for 1% -> 0% of each run, Pallas kernels for 0% -> 0%
where the time goes in v1:
time: 133 us
  Pallas kernels  125 us (94%)
  local copies, waits for them, and re-layouts  7.79 us (6%)
    pallas_call x1, Pallas kernels, body(): pl.pallas_call(functools.partial(kernel, rows_n, cols_n), out_shape=(jax....  125 us
    unnamed x4, local copies, waits for them, and re-layouts  7.79 us

profile of v1, /device:TPU:0, one launch (start us, length us, event | category | flops | bytes accessed | tf_op | source)
XLA Modules:
  0.0 133.2 jit_solution(14548515694796765869)
XLA Ops:
  0.6 1.3 %copy.7.struct_ref = s32[8,3]{1,0:T(8,128)} copy(s32[8,3]{0,1:T(4,128)} %param.7) | data formatting | bytes 192 | tf_op args[3]
  2.0 2.1 %copy.10 = f32[128,1,3,512]{3,0,2,1:T(8,128)} copy(f32[128,1,3,512]{3,1,2,0:T(1,128)} %param.5) | data formatting | bytes 1572864 | tf_op args[1]
  4.1 124.8 %shard_map.59 = (f32[3,128,512]{2,1,0:T(8,128)}, f32[3,64,128]{2,1,0:T(8,128)}) custom-call(s32[8,3]{1,0:T(8,128)} %copy.7.struct_ref, f32[3,128,512]{2,1,0:T(8,128)} %bitcast.8, f32[1,2,512,512]{3,2,1,0:T(8,128)} %inverse_ref.1, f32[3,64,128]{2,1,0:T(8,128)} %pivot_ref.1), custom_call_target="tpu_custom_call" | custom-call | tf_op jit(solution)/shard_map/pallas_call | solution.py:334
  128.8 2.8 %copy.8 = f32[128,1,3,512]{3,1,2,0:T(1,128)} copy(f32[128,1,3,512]{3,0,2,1:T(8,128)} %bitcast.9) | data formatting | bytes 1572864
  131.6 1.5 %copy.12 = f32[3,64,128]{2,1,0:T(8,128)} copy(f32[3,64,128]{2,1,0:T(8,128)} %get-tuple-element.11) | data formatting | bytes 196608

commit v2 on v1

--- a/solution.py
+++ b/solution.py
@@ -9,6 +9,7 @@
 
 MESH = pl.DeviceIdType.MESH
 PAIR = 2
+HALVES = 2
 
 
 def split(value):
@@ -64,7 +65,8 @@
 ):
     row = lax.axis_index("prow")
     col = lax.axis_index("pcol")
-    supers = factor_ref.shape[0]
+    chunks = factor_ref.shape[0]
+    supers = chunks // HALVES
     members, width = a_full.shape[0], a_full.shape[1]
     rows = factor_ref.shape[1]
     chips = rows_n // PAIR
@@ -196,7 +198,7 @@
         collect(k)
 
         def convert(index, carry):
-            mask = struct_ref[col * members + index // cols_n, k].astype(jnp.float32)
+            mask = struct_ref[col * members + index // cols_n, k // HALVES].astype(jnp.float32)
             high, low = split(columns[k, index] * mask)
             at = pl.ds(pl.multiple_of(index * rows, rows), rows)
             l_high[at, :] = high
@@ -249,16 +251,16 @@
     def finish_panel(k):
         ring_copy(k, cols_n - 2).wait_recv()
         block = pl.ds(pl.multiple_of(col * rows, rows), rows)
-        mask = struct_ref[row, k].astype(jnp.float32)
+        mask = struct_ref[row, k // HALVES].astype(jnp.float32)
         result = -mask * (partial[k, block, :] + ring_in[k, cols_n - 2])
         panel_ref[k] = result
-        f_high, f_low = split(factor_ref[k] * mask)
         r_high, r_low = split(result)
-        for at in range(rows_n):
-            these = slice(at * part, (at + 1) * part)
-            terms[k, at % PAIR, at // PAIR] = dot3(
-                f_high[:, these], f_low[:, these], r_high, r_low, ((0,), (0,))
-            )
+        for half in range(HALVES):
+            f_high, f_low = split(factor_ref[k // HALVES * HALVES + half] * mask)
+            term = dot3(f_high, f_low, r_high, r_low, ((0,), (0,)))
+            for here in range(rows_n // HALVES):
+                at = half * (rows_n // HALVES) + here
+                terms[k, at % PAIR, at // PAIR] = term[here * part : (here + 1) * part]
         copy = pair_copy(k)
         copy.start()
         sent.append(copy)
@@ -276,26 +278,30 @@
         for step in range(1, chips):
             chip_copy(k, step).wait_recv()
             total = total + chip_in[k, step - 1]
-        for at in range(cols_n):
-            cut[k, at] = total[:, at * lanes : (at + 1) * lanes]
-        for step in range(cols_n - 1, 0, -1):
-            copy = cut_copy(k, step)
-            copy.start()
-            sent.append(copy)
+        for at in range(cols_n // HALVES):
+            cut[k // HALVES, k % HALVES * (cols_n // HALVES) + at] = total[:, at * lanes : (at + 1) * lanes]
+        if k % HALVES == HALVES - 1:
+            for step in range(cols_n - 1, 0, -1):
+                copy = cut_copy(k // HALVES, step)
+                copy.start()
+                sent.append(copy)
 
     def add_cuts(k):
-        total = cut[k, col]
+        if k % HALVES < HALVES - 1:
+            return
+        at = k // HALVES
+        total = cut[at, col]
         for step in range(1, cols_n):
-            cut_copy(k, step).wait_recv()
-            total = total + cut_in[k, step - 1]
-        diag_ref[k] = pivot_ref[k] - total
+            cut_copy(at, step).wait_recv()
+            total = total + cut_in[at, step - 1]
+        diag_ref[at] = pivot_ref[at] - total
 
     load = pltpu.make_async_copy(inverse_ref.at[0], a_full, a_sem)
     load.start()
-    for k in range(supers):
+    for k in range(chunks):
         across(k).start()
         sent.append(across(k))
-    for k in range(supers):
+    for k in range(chunks):
         across(k).wait_recv()
         along(k).start()
         sent.append(along(k))
@@ -310,12 +316,12 @@
     for step in range(1, cols_n - 1):
         stages.append(functools.partial(lambda at, k: ring_step(k, at), step))
     stages += [finish_panel, add_pair, add_chips, add_cuts]
-    for wave in range(supers + len(stages) - 1):
-        if wave < supers:
-            if wave + 1 < supers:
+    for wave in range(chunks + len(stages) - 1):
+        if wave < chunks:
+            if wave + 1 < chunks:
                 start_spread(wave + 1)
             forward(wave)
-        for k in range(supers):
+        for k in range(chunks):
             if 0 <= wave - k < len(stages):
                 stages[wave - k](k)
 
@@ -328,13 +334,14 @@
     members, width = ancestor_inverse.shape[1], ancestor_inverse.shape[3]
     rows, _, supers, _ = factor_panel.shape
     chips, part, lanes = rows_n // PAIR, width // rows_n, width // cols_n
-    factor = jnp.transpose(factor_panel[:, 0], (1, 0, 2))
+    chunks, piece = supers * HALVES, width // HALVES
+    factor = jnp.transpose(factor_panel.reshape(rows, chunks, piece), (1, 0, 2))
     f32, b16, dma = jnp.float32, jnp.bfloat16, pltpu.SemaphoreType.DMA
     vmem = pl.BlockSpec(memory_space=pltpu.VMEM)
     panel, diagonal = pl.pallas_call(
         functools.partial(kernel, rows_n, cols_n),
         out_shape=(
-            jax.ShapeDtypeStruct((supers, rows, width), f32),
+            jax.ShapeDtypeStruct((chunks, rows, piece), f32),
             jax.ShapeDtypeStruct(pivot_inverse.shape, f32),
         ),
         in_specs=[
@@ -348,29 +355,29 @@
             pltpu.VMEM((members, width, width), f32),
             pltpu.VMEM((width, members * width), b16),
             pltpu.VMEM((width, members * width), b16),
-            pltpu.VMEM((supers, rows, width), f32),
-            pltpu.VMEM((supers, members * cols_n, rows, width), f32),
-            pltpu.VMEM((members * width, width), b16),
-            pltpu.VMEM((members * width, width), b16),
-            pltpu.VMEM((supers, width, width), f32),
-            pltpu.VMEM((supers, cols_n - 1, rows, width), f32),
-            pltpu.VMEM((supers, PAIR, chips, part, width), f32),
-            pltpu.VMEM((supers, chips, part, width), f32),
-            pltpu.VMEM((supers, chips, part, width), f32),
-            pltpu.VMEM((supers, chips - 1, part, width), f32),
+            pltpu.VMEM((chunks, rows, piece), f32),
+            pltpu.VMEM((chunks, members * cols_n, rows, piece), f32),
+            pltpu.VMEM((members * width, piece), b16),
+            pltpu.VMEM((members * width, piece), b16),
+            pltpu.VMEM((chunks, width, piece), f32),
+            pltpu.VMEM((chunks, cols_n - 1, rows, piece), f32),
+            pltpu.VMEM((chunks, PAIR, chips, part, piece), f32),
+            pltpu.VMEM((chunks, chips, part, piece), f32),
+            pltpu.VMEM((chunks, chips, part, piece), f32),
+            pltpu.VMEM((chunks, chips - 1, part, piece), f32),
             pltpu.VMEM((supers, cols_n, part, lanes), f32),
             pltpu.VMEM((supers, cols_n - 1, part, lanes), f32),
             dma,
-            dma((2, supers)),
-            dma((2, supers)),
-            dma((supers, 2 * chips)),
-            dma((supers, 2 * chips)),
-            dma((supers, cols_n - 1)),
-            dma((supers, cols_n - 1)),
-            dma((supers,)),
-            dma((supers,)),
-            dma((supers, chips - 1)),
-            dma((supers, chips - 1)),
+            dma((2, chunks)),
+            dma((2, chunks)),
+            dma((chunks, 2 * chips)),
+            dma((chunks, 2 * chips)),
+            dma((chunks, cols_n - 1)),
+            dma((chunks, cols_n - 1)),
+            dma((chunks,)),
+            dma((chunks,)),
+            dma((chunks, chips - 1)),
+            dma((chunks, chips - 1)),
             dma((supers, cols_n - 1)),
             dma((supers, cols_n - 1)),
         ],
@@ -378,7 +385,7 @@
             collective_id=0, has_side_effects=True, vmem_limit_bytes=56 * 1024 * 1024
         ),
     )(structure, factor, ancestor_inverse, pivot_inverse)
-    return jnp.transpose(panel, (1, 0, 2))[:, None], diagonal
+    return jnp.transpose(panel, (1, 0, 2)).reshape(factor_panel.shape), diagonal
 
 
 def solution(mesh):

time: 133 us -> 117 us (0.88)
  Pallas kernels: 125 us -> 108 us
    pallas_call x1, Pallas kernels: 125 us -> 108 us  [body(): pl.pallas_call(functools.partial(kernel, rows_n, cols_n), out_shape=(jax....]
    unnamed x4 -> x6, local copies, waits for them, and re-layouts: 7.79 us -> 5.9 us
    transpose x0 -> x1, local copies, waits for them, and re-layouts: none -> 1.42 us  [body(): jnp.transpose(panel, (1, 0, 2)).reshape(factor_panel.shape)]
where the time goes in v2:
time: 117 us
  Pallas kernels  108 us (92%)
  local copies, waits for them, and re-layouts  8.47 us (7%)
    pallas_call x1, Pallas kernels, body(): pl.pallas_call(functools.partial(kernel, rows_n, cols_n), out_shape=(jax....  108 us
    unnamed x6, local copies, waits for them, and re-layouts  5.9 us

profile of v2, /device:TPU:0, one launch (start us, length us, event | category | flops | bytes accessed | tf_op | source)
XLA Modules:
  0.0 116.8 jit_solution(9126128398416141245)
XLA Ops:
  0.6 1.3 %copy.9.struct_ref = s32[8,3]{1,0:T(8,128)} copy(s32[8,3]{0,1:T(4,128)} %param.7) | data formatting | bytes 192 | tf_op args[3]
  2.0 2.2 %copy.7 = f32[128,1,3,512]{0,3,2,1:T(8,128)S(1)} copy(f32[128,1,3,512]{3,1,2,0:T(1,128)} %param.5) | data formatting | bytes 1572864 | tf_op args[1]
  4.2 1.1 copy.8
  5.3 107.6 %shard_map.59 = (f32[6,128,256]{2,1,0:T(8,128)}, f32[3,64,128]{2,1,0:T(8,128)}) custom-call(s32[8,3]{1,0:T(8,128)} %copy.9.struct_ref, f32[6,128,256]{2,1,0:T(8,128)} %bitcast.6, f32[1,2,512,512]{3,2,1,0:T(8,128)} %inverse_ref.1, f32[3,64,128]{2,1,0:T(8,128)} %pivot_ref.1), custom_call_target="tpu_custom_call" | custom-call | tf_op jit(solution)/shard_map/pallas_call | solution.py:341
  113.0 0.0 copy-start
  113.0 1.4 %copy.10 = f32[128,6,256]{0,2,1:T(8,128)S(1)} copy(f32[128,6,256]{2,0,1:T(8,128)} %bitcast.7) | data formatting | bytes 1572864 | tf_op jit(solution)/shard_map/transpose | solution.py:388
  114.4 1.7 %copy.11 = f32[128,1,3,512]{3,1,2,0:T(1,128)} copy(f32[128,1,3,512]{0,3,2,1:T(8,128)S(1)} %bitcast.4) | data formatting | bytes 1572864
  116.1 0.0 copy-done
  116.1 0.6 copy.13
Async XLA Ops:
  113.0 3.2 %copy-start = (f32[3,64,128]{2,1,0:T(8,128)S(1)}, f32[3,64,128]{2,1,0:T(8,128)}, u32[]{:S(2)}) copy-start(f32[3,64,128]{2,1,0:T(8,128)} %get-tuple-element.11) | copy-start | bytes 294916
